TPU v7x, 32 devices: a whole 2x2x4 slice. The times are simulated.
32 devices in a mesh: grp: 4 (over z), freq: 8 (over y, x, core).
Axes of the slice: x: 2, y: 2, z: 4, core: 2. Of those that a mesh axis runs over, the one named last changes fastest.
Arguments:
- sources: bfloat16 [1024, 32768], P('freq', 'grp'), may hold values from -6 to 6
- panel_pos: float32 [3, 32768], P(None, 'grp'), may hold values from -1 to 1
- panel_blade: int32 [32768], P('grp'), may hold values from 0 to 3
- observer_table: float32 [3, 2048], replicated, may hold values from -8 to 8, as said below
- observer_index: int32 [32], replicated, may hold values from 0 to 2047
Outputs:
- spectra: float32 [512, 4, 2, 32], P('freq', 'grp')
Inputs may be any that keep to these rules, and one draw needn't show every extreme that they name: `observer_table`: each observer lies 3 to 8 units from the anchor (0, 0, 0).
All inputs are finite; a program needn't handle non-finite values.
Results may differ from a plain program's by a relative error of at most 0.0047.
Values may be sent and summed in bfloat16 or wider, within the bound.
A program may use at most 64 MiB of HBM per device.

v0:
```python
import math
import jax
import jax.numpy as jnp
from jax import lax
from jax.sharding import PartitionSpec as P

NT = 1024
NF = 512
NCOMP = 4
wave_step = 0.04


def transform_table():
    row_index = jnp.arange(2 * NF, dtype=jnp.int32)
    samples = jnp.arange(NT, dtype=jnp.int32)
    frequency = row_index // 2
    parity = row_index % 2
    turn_count = frequency[:, None] * samples[None, :] % NT
    angle_table = 2.0 * math.pi / NT * turn_count.astype(jnp.float32)
    values = jnp.where(parity[:, None] == 0, jnp.cos(angle_table), -jnp.sin(angle_table))
    return (values / math.sqrt(NT)).astype(jnp.bfloat16)


def distances(positions, observers):
    offset_x = observers[0][:, None] - positions[0][None, :]
    offset_y = observers[1][:, None] - positions[1][None, :]
    offset_z = observers[2][:, None] - positions[2][None, :]
    return jnp.sqrt(offset_x * offset_x + offset_y * offset_y + offset_z * offset_z)


def blade_masks(blades):
    return (blades[None, :] == jnp.arange(NCOMP, dtype=jnp.int32)[:, None]).astype(jnp.bfloat16)


def frequency_term(frequency, spectrum_pair, blade_mask, distance, amplitude):
    wavenumber = wave_step * frequency.astype(jnp.float32)
    phase_angle = wavenumber * distance
    green_matrix = jnp.concatenate(
        [jnp.cos(phase_angle) * amplitude, -jnp.sin(phase_angle) * amplitude], axis=0
    ).astype(jnp.bfloat16)
    weighted = jnp.concatenate(
        [spectrum_pair[0][None, :] * blade_mask, spectrum_pair[1][None, :] * blade_mask], axis=0
    )
    product = lax.dot_general(
        weighted, green_matrix, (((1,), (1,)), ((), ())), preferred_element_type=jnp.float32
    )
    blade_count = blade_mask.shape[0]
    observer_count = distance.shape[0]
    real_part = product[:blade_count, :observer_count] - product[blade_count:, observer_count:]
    imag_part = product[:blade_count, observer_count:] + product[blade_count:, :observer_count]
    return jnp.stack([real_part, imag_part], axis=1)


def body(sources, panel_pos, panel_blade, observer_table, observer_index):
    freq_share = NF // lax.axis_size("freq")
    position = lax.axis_index("freq")
    observers = observer_table[:, observer_index]
    dft_table = transform_table()
    device_count = lax.axis_size("freq")
    shaped = sources.reshape(sources.shape[0], device_count, sources.shape[1] // device_count)
    piece = lax.all_to_all(shaped, "freq", split_axis=1, concat_axis=0, tiled=True)
    item_count = piece.shape[2]
    flat = piece.reshape(piece.shape[0], item_count)
    local_spec = jnp.dot(dft_table, flat, preferred_element_type=jnp.float32).astype(jnp.bfloat16)
    gathered = lax.all_to_all(
        local_spec.reshape(2 * NF, 1, item_count), "freq", split_axis=0, concat_axis=1, tiled=True
    )
    received = gathered.reshape(gathered.shape[0], gathered.shape[1] * gathered.shape[2])
    spectra_pairs = received.reshape(freq_share, 2, received.shape[1])
    distance = distances(panel_pos, observers)
    amplitude = 0.25 / (math.pi * distance)
    blade_mask = blade_masks(panel_blade)
    frequencies = position * freq_share + jnp.arange(freq_share, dtype=jnp.int32)

    def per_frequency(element):
        return frequency_term(element[0], element[1], blade_mask, distance, amplitude)

    partial_value = lax.map(per_frequency, (frequencies, spectra_pairs))
    summed = lax.psum(partial_value, "grp")
    blade_share = NCOMP // lax.axis_size("grp")
    return lax.dynamic_slice_in_dim(summed, lax.axis_index("grp") * blade_share, blade_share, 1)


def solution(mesh):
    in_specs = (P("freq", "grp"), P(None, "grp"), P("grp"), P(), P())
    out_specs = P("freq", "grp", None, None)
    return jax.shard_map(body, mesh=mesh, in_specs=in_specs, out_specs=out_specs, check_vma=False)
```

profile of v0, /device:TPU:0, one launch (start us, length us, event | category | flops | bytes accessed | tf_op | source)
XLA Modules:
  0.0 632.9 jit_solution(9008926720111402404)
XLA Ops:
  10.6 5.2 all-to-all-start
  17.1 25.4 %all-to-all-done = bf16[128,8,1024]{0,2,1:T(8,128)(2,1)S(1)} async-done(((bf16[128,8,1024]{0,2,1:T(8,128)(2,1)}), bf16[128,8,1024]{0,2,1:T(8,128)(2,1)S(1)}, u32[]{:S(2)}, u32[]{:S(2)}) %all-to-all-start) | async-done | bytes 2097184 | tf_op jit(solution)/shard_map/all_to_all | solution.py:61
  45.1 22.1 %convert_bitcast_fusion = bf16[1024,1,1024]{2,0,1:T(8,128)(2,1)} fusion(bf16[1024,1024]{1,0:T(8,128)(2,1)} %bitcast.37, s32[1024]{0:T(1024)S(1)} %add_select_fusion.1, pred[1024]{0:T(1024)(128)(4,1)S(1)} %fusion.32), kind=kOutput, calls=%fused_computation.37 | convolution fusion | flops 2167406592 | bytes 4199424 | tf_op jit(solution)/shard_map/dot_general | solution.py:64
  79.4 26.2 %all-to-all-done.1 = bf16[8,2,65536]{2,1,0:T(2,128)(2,1)S(1)} async-done(((bf16[8,2,65536]{2,1,0:T(2,128)(2,1)}), bf16[8,2,65536]{2,1,0:T(2,128)(2,1)S(1)}, u32[]{:S(2)}, u32[]{:S(2)}) %all-to-all-start.1) | async-done | bytes 2097184 | tf_op jit(solution)/shard_map/all_to_all | solution.py:65
  117.0 472.7 %while.12 = (s32[]{:T(128)}, f32[64,4,2,32]{3,1,2,0:T(4,128)S(1)}, bf16[64,2,8192]{2,1,0:T(2,128)(2,1)}, s32[64]{0:T(128)S(1)}, s32[8192]{0:T(1024)S(1)}, /*inde...) while((s32[]{:T(128)}, f32[64,4,2,32]{3,1,2,0:T(4,128)S(1)}, ...), condition=%wide.region_1.2_spmd.clone.clone, body=%wide.region_0.1_spmd.clone.clone.sunk | while | flops 15041029 | bytes 2602569 | solution.py:78
  118.2 4.6 multiply_convert_fusion.7
  125.6 4.6 multiply_convert_fusion.7
  132.9 4.6 multiply_convert_fusion.7
  140.3 4.6 multiply_convert_fusion.7
  147.7 4.6 multiply_convert_fusion.7
  155.1 4.6 multiply_convert_fusion.7
  162.5 4.6 multiply_convert_fusion.7
  169.9 4.6 multiply_convert_fusion.7
  177.3 4.6 multiply_convert_fusion.7
  184.7 4.6 multiply_convert_fusion.7
  192.0 4.6 multiply_convert_fusion.7
  199.4 4.6 multiply_convert_fusion.7
  206.8 4.6 multiply_convert_fusion.7
  214.2 4.6 multiply_convert_fusion.7
  221.6 4.6 multiply_convert_fusion.7
  229.0 4.6 multiply_convert_fusion.7
  236.4 4.6 multiply_convert_fusion.7
  243.7 4.6 multiply_convert_fusion.7
  251.1 4.6 multiply_convert_fusion.7
  258.5 4.6 multiply_convert_fusion.7
  265.9 4.6 multiply_convert_fusion.7
  273.3 4.6 multiply_convert_fusion.7
  280.7 4.6 multiply_convert_fusion.7
  288.1 4.6 multiply_convert_fusion.7
  295.4 4.6 multiply_convert_fusion.7
  302.8 4.6 multiply_convert_fusion.7
  325.0 4.6 multiply_convert_fusion.7
  332.4 4.6 multiply_convert_fusion.7
  354.5 4.6 multiply_convert_fusion.7
  361.9 4.6 multiply_convert_fusion.7
  391.5 4.6 multiply_convert_fusion.7
  398.9 4.6 multiply_convert_fusion.7
  428.4 4.6 multiply_convert_fusion.7
  435.8 4.6 multiply_convert_fusion.7
  465.3 4.6 multiply_convert_fusion.7
  472.7 4.6 multiply_convert_fusion.7
  494.9 4.6 multiply_convert_fusion.7
  502.3 4.6 multiply_convert_fusion.7
  531.8 4.6 multiply_convert_fusion.7
  539.2 4.6 multiply_convert_fusion.7
  568.7 4.6 multiply_convert_fusion.7
  576.1 4.6 multiply_convert_fusion.7
  590.5 34.2 %all-reduce.2.cloned.1.call-done = f32[64,4,2,32]{0,3,2,1:T(8,128)} async-done(((f32[64,4,2,32]{0,3,2,1:T(8,128)}), f32[64,4,2,32]{0,3,2,1:T(8,128)}) %all-reduce.2.cloned.1.call-update) | async-done | bytes 65552 | tf_op jit(solution)/shard_map/psum | solution.py:79
  (438 shorter events, 272.5 us)
Async XLA Ops:
  6.5 9.3 %copy-start.2 = (f32[3,2048]{1,0:T(4,128)S(1)}, f32[3,2048]{1,0:T(4,128)}, u32[]{:S(2)}) copy-start(f32[3,2048]{1,0:T(4,128)} %param.10) | copy-start | bytes 73732
  6.5 9.7 %copy-start.3 = (s32[32]{0:T(128)S(1)}, s32[32]{0:T(128)}, u32[]{:S(2)}) copy-start(s32[32]{0:T(128)} %param.11) | copy-start | bytes 388
  10.6 31.8 %all-to-all-start = ((bf16[128,8,1024]{0,2,1:T(8,128)(2,1)}), bf16[128,8,1024]{0,2,1:T(8,128)(2,1)S(1)}, u32[]{:S(2)}, u32[]{:S(2)}) async-start(bf16[128,8,1024]{0,2,1:T(8,128)(2,1)} %bitcast.36), calls=%async_computation | async-start | bytes 4194304 | tf_op jit(solution)/shard_map/all_to_all | solution.py:61
  71.6 7.7 %copy-start.1 = (f32[3,8192]{1,0:T(4,128)S(1)}, f32[3,8192]{1,0:T(4,128)}, u32[]{:S(2)}) copy-start(f32[3,8192]{1,0:T(4,128)} %param.8) | copy-start | bytes 294916
  75.4 30.2 %all-to-all-start.1 = ((bf16[8,2,65536]{2,1,0:T(2,128)(2,1)}), bf16[8,2,65536]{2,1,0:T(2,128)(2,1)S(1)}, u32[]{:S(2)}, u32[]{:S(2)}) async-start(bf16[8,2,65536]{2,1,0:T(2,128)(2,1)} %reshape.63), calls=%async_computation.1 | async-start | bytes 4194304 | tf_op jit(solution)/shard_map/all_to_all | solution.py:65
  79.1 545.6 %all-reduce.2.cloned.1.call-start = ((), (), s32[]{:S(2)}) async-start(), calls=%async_computation.2 | async-start | bytes 262144 | tf_op jit(solution)/shard_map/psum | solution.py:79
  113.0 4.0 copy-start
Sparse Core Ops, SparseCore 0:
  590.6 34.0 all-reduce.1
where the time goes:
time: 639 us; the launch traced here: 633 us
  other arithmetic  307 us (48%)
  local copies, waits for them, and re-layouts  130 us (20%)
  waiting for transfers between devices  85.8 us (13%)
  matrix products  46 us (7%)
  loops' own time  41.1 us (6%)
  between operations  13.5 us (2%)
  starting transfers between devices  9.02 us (1%)
    another operation x64, other arithmetic  294 us
    slice x64, local copies, waits for them, and re-layouts, frequency_term(): spectrum_pair[0][None, :] * blade_mask  65.3 us
    another operation x1, loops' own time, body(): partial_value = lax.map(per_frequency, (frequencies, spectra_pairs))  41.1 us
    dynamic_slice x64, local copies, waits for them, and re-layouts, body(): partial_value = lax.map(per_frequency, (frequencies, spectra_pairs))  38.9 us
    psum x1, waiting for transfers between devices, body(): summed = lax.psum(partial_value, 'grp')  34.2 us
    all_to_all x1, waiting for transfers between devices, body(): lax.all_to_all(local_spec.reshape(2 * NF, 1, item_count), 'freq', split_a...  26.2 us
    all_to_all x1, waiting for transfers between devices, body(): lax.all_to_all(shaped, 'freq', split_axis=1, concat_axis=0, tiled=True)  25.4 us
    dot_general x64, matrix products, frequency_term(): lax.dot_general(weighted, green_matrix, (((1,), (1,)), ((), ())), preferr...  23.9 us
  transfers between devices with their start and end apart: 3, of which 3 were waited for; matrix products, arithmetic and copies ran while one was open for 0% of the time, Pallas kernels for 0%

commit v1 on v0

--- a/solution.py
+++ b/solution.py
@@ -76,7 +76,8 @@
         return frequency_term(element[0], element[1], blade_mask, distance, amplitude)
 
     partial_value = lax.map(per_frequency, (frequencies, spectra_pairs))
-    summed = lax.psum(partial_value, "grp")
+    parts = lax.all_gather(partial_value, "grp")
+    summed = jnp.sum(parts, axis=0)
     blade_share = NCOMP // lax.axis_size("grp")
     return lax.dynamic_slice_in_dim(summed, lax.axis_index("grp") * blade_share, blade_share, 1)
 

time: 639 us -> 612 us (0.958)
  waiting for transfers between devices: 85.8 us -> 51.6 us
  blocking collectives: 0 us -> 21.5 us
  between operations: 13.5 us -> 0.15 us
    psum x1 -> x0, waiting for transfers between devices: 34.2 us -> none  [body(): summed = lax.psum(partial_value, 'grp')]
    all_gather x0 -> x1, blocking collectives: none -> 21.5 us  [body(): parts = lax.all_gather(partial_value, 'grp')]
  transfers between devices with their start and end apart: 3 -> 2, of which waited for: 3 -> 2; matrix products, arithmetic and copies ran while one was open for 0% -> 0% of each run, Pallas kernels for 0% -> 0%
where the time goes in v1:
time: 612 us; the launch traced here: 606 us
  other arithmetic  308 us (50%)
  local copies, waits for them, and re-layouts  129 us (21%)
  waiting for transfers between devices  51.6 us (8%)
  matrix products  46 us (8%)
  loops' own time  41.1 us (7%)
  blocking collectives  21.5 us (4%)
  starting transfers between devices  9 us (1%)
    another operation x64, other arithmetic  294 us
    slice x64, local copies, waits for them, and re-layouts, frequency_term(): spectrum_pair[0][None, :] * blade_mask  65.3 us
    another operation x1, loops' own time, body(): partial_value = lax.map(per_frequency, (frequencies, spectra_pairs))  41.1 us
    dynamic_slice x64, local copies, waits for them, and re-layouts, body(): partial_value = lax.map(per_frequency, (frequencies, spectra_pairs))  38.9 us
    all_to_all x1, waiting for transfers between devices, body(): lax.all_to_all(local_spec.reshape(2 * NF, 1, item_count), 'freq', split_a...  26.3 us
    all_to_all x1, waiting for transfers between devices, body(): lax.all_to_all(shaped, 'freq', split_axis=1, concat_axis=0, tiled=True)  25.4 us
    dot_general x64, matrix products, frequency_term(): lax.dot_general(weighted, green_matrix, (((1,), (1,)), ((), ())), preferr...  23.8 us
    dot_general x1, matrix products, body(): jnp.dot(dft_table, flat, preferred_element_type=jnp.float32)  22.1 us
  transfers between devices with their start and end apart: 2, of which 2 were waited for; matrix products, arithmetic and copies ran while one was open for 0% of the time, Pallas kernels for 0%

profile of v1, /device:TPU:0, one launch (start us, length us, event | category | flops | bytes accessed | tf_op | source)
XLA Modules:
  0.0 605.7 jit_solution(17875584492578940822)
XLA Ops:
  4.1 5.2 all-to-all-start
  10.6 25.4 %all-to-all-done = bf16[128,8,1024]{0,2,1:T(8,128)(2,1)S(1)} async-done(((bf16[128,8,1024]{0,2,1:T(8,128)(2,1)}), bf16[128,8,1024]{0,2,1:T(8,128)(2,1)S(1)}, u32[]{:S(2)}, u32[]{:S(2)}) %all-to-all-start) | async-done | bytes 2097184 | tf_op jit(solution)/shard_map/all_to_all | solution.py:61
  38.5 22.1 %convert_bitcast_fusion = bf16[1024,1,1024]{2,0,1:T(8,128)(2,1)} fusion(bf16[1024,1024]{1,0:T(8,128)(2,1)} %bitcast.39, s32[1024]{0:T(1024)S(1)} %add_select_fusion.1, pred[1024]{0:T(1024)(128)(4,1)S(1)} %fusion.32), kind=kOutput, calls=%fused_computation.37 | convolution fusion | flops 2167406592 | bytes 4199424 | tf_op jit(solution)/shard_map/dot_general | solution.py:64
  72.8 26.3 %all-to-all-done.1 = bf16[8,2,65536]{2,1,0:T(2,128)(2,1)S(1)} async-done(((bf16[8,2,65536]{2,1,0:T(2,128)(2,1)}), bf16[8,2,65536]{2,1,0:T(2,128)(2,1)S(1)}, u32[]{:S(2)}, u32[]{:S(2)}) %all-to-all-start.1) | async-done | bytes 2097184 | tf_op jit(solution)/shard_map/all_to_all | solution.py:65
  110.4 472.7 %while.12 = (s32[]{:T(128)}, f32[64,4,2,32]{3,1,2,0:T(4,128)S(1)}, bf16[64,2,8192]{2,1,0:T(2,128)(2,1)}, s32[64]{0:T(128)S(1)}, s32[8192]{0:T(1024)S(1)}, /*inde...) while((s32[]{:T(128)}, f32[64,4,2,32]{3,1,2,0:T(4,128)S(1)}, ...), condition=%wide.region_1.2_spmd.clone.clone, body=%wide.region_0.1_spmd.clone.clone.sunk | while | flops 15041029 | bytes 2602569 | solution.py:78
  111.7 4.6 multiply_convert_fusion.7
  119.0 4.6 multiply_convert_fusion.7
  126.4 4.6 multiply_convert_fusion.7
  133.8 4.6 multiply_convert_fusion.7
  141.2 4.6 multiply_convert_fusion.7
  148.6 4.6 multiply_convert_fusion.7
  156.0 4.6 multiply_convert_fusion.7
  163.4 4.6 multiply_convert_fusion.7
  170.7 4.6 multiply_convert_fusion.7
  178.1 4.6 multiply_convert_fusion.7
  185.5 4.6 multiply_convert_fusion.7
  192.9 4.6 multiply_convert_fusion.7
  200.3 4.6 multiply_convert_fusion.7
  207.7 4.6 multiply_convert_fusion.7
  215.1 4.6 multiply_convert_fusion.7
  222.5 4.6 multiply_convert_fusion.7
  229.8 4.6 multiply_convert_fusion.7
  237.2 4.6 multiply_convert_fusion.7
  244.6 4.6 multiply_convert_fusion.7
  252.0 4.6 multiply_convert_fusion.7
  259.4 4.6 multiply_convert_fusion.7
  266.8 4.6 multiply_convert_fusion.7
  274.2 4.6 multiply_convert_fusion.7
  281.5 4.6 multiply_convert_fusion.7
  288.9 4.6 multiply_convert_fusion.7
  296.3 4.6 multiply_convert_fusion.7
  303.7 4.6 multiply_convert_fusion.7
  311.1 4.6 multiply_convert_fusion.7
  333.2 4.6 multiply_convert_fusion.7
  340.6 4.6 multiply_convert_fusion.7
  370.2 4.6 multiply_convert_fusion.7
  377.6 4.6 multiply_convert_fusion.7
  407.1 4.6 multiply_convert_fusion.7
  414.5 4.6 multiply_convert_fusion.7
  444.0 4.6 multiply_convert_fusion.7
  451.4 4.6 multiply_convert_fusion.7
  473.6 4.6 multiply_convert_fusion.7
  481.0 4.6 multiply_convert_fusion.7
  510.5 4.6 multiply_convert_fusion.7
  517.9 4.6 multiply_convert_fusion.7
  547.5 4.6 multiply_convert_fusion.7
  554.8 4.6 multiply_convert_fusion.7
  583.2 21.5 %all-gather = f32[256,4,2,32]{3,1,2,0:T(4,128)S(1)} all-gather(f32[64,4,2,32]{3,1,2,0:T(4,128)S(1)} %get-tuple-element.42), channel_id=2, replica_groups=mesh['grp'=4,'freq'=8] {'grp'}, dimensions={0}, use_global_device_ids=true | all-gather | bytes 327680 | tf_op jit(solution)/shard_map/all_gather | solution.py:79
  (437 shorter events, 271.4 us)
Async XLA Ops:
  0.0 9.3 %copy-start.2 = (f32[3,2048]{1,0:T(4,128)S(1)}, f32[3,2048]{1,0:T(4,128)}, u32[]{:S(2)}) copy-start(f32[3,2048]{1,0:T(4,128)} %param.10) | copy-start | bytes 73732
  0.0 9.7 %copy-start.3 = (s32[32]{0:T(128)S(1)}, s32[32]{0:T(128)}, u32[]{:S(2)}) copy-start(s32[32]{0:T(128)} %param.11) | copy-start | bytes 388
  4.1 31.8 %all-to-all-start = ((bf16[128,8,1024]{0,2,1:T(8,128)(2,1)}), bf16[128,8,1024]{0,2,1:T(8,128)(2,1)S(1)}, u32[]{:S(2)}, u32[]{:S(2)}) async-start(bf16[128,8,1024]{0,2,1:T(8,128)(2,1)} %bitcast.37), calls=%async_computation | async-start | bytes 4194304 | tf_op jit(solution)/shard_map/all_to_all | solution.py:61
  65.1 7.6 %copy-start.1 = (f32[3,8192]{1,0:T(4,128)S(1)}, f32[3,8192]{1,0:T(4,128)}, u32[]{:S(2)}) copy-start(f32[3,8192]{1,0:T(4,128)} %param.8) | copy-start | bytes 294916
  68.9 30.2 %all-to-all-start.1 = ((bf16[8,2,65536]{2,1,0:T(2,128)(2,1)}), bf16[8,2,65536]{2,1,0:T(2,128)(2,1)S(1)}, u32[]{:S(2)}, u32[]{:S(2)}) async-start(bf16[8,2,65536]{2,1,0:T(2,128)(2,1)} %reshape.64), calls=%async_computation.1 | async-start | bytes 4194304 | tf_op jit(solution)/shard_map/all_to_all | solution.py:65
  106.5 4.0 copy-start
